TPU v7x, 512 devices: a 8x2x16 block of a 8x8x16 slice. The times are simulated.
512 devices in a mesh: grp: 2 (over y), ep: 128 (over x, z), tp: 2 (over core).
Axes of the slice: x: 8, y: 2, z: 16, core: 2. Of those that a mesh axis runs over, the one named last changes fastest.
The devices are a block of a 8x8x16 slice.
Arguments:
- queries: bfloat16 [16384, 16, 576], P(('grp', 'ep'), 'tp'), parts along dimension 0, may hold values from -450 to 450
- latent_cache: bfloat16 [768, 512, 576], P(('grp', 'ep'), 'tp'), parts along dimension 0, may hold values from -6 to 6
- residual: bfloat16 [16384, 2048], P(('grp', 'ep')), parts along dimension 0, may hold values from -8 to 8
- token_request: int32 [16384], P(('grp', 'ep')), parts along dimension 0, may hold values from 0 to 2, as said below
- token_visible: int32 [16384], P(('grp', 'ep')), parts along dimension 0, may hold values from 1 to 512, as said below
- value_proj: bfloat16 [16, 512, 128], P('tp', 'ep'), may hold values from -0.25 to 0.25
- out_proj: bfloat16 [2048, 2048], P('tp', 'ep'), may hold values from -0.125 to 0.125
- norm_gain: float32 [2048], replicated, may hold values from 0.1 to 1.9
- router: bfloat16 [2048, 64], replicated, may hold values from -0.0390625 to 0.0390625
- expert_ids: int32 [16384, 6], P(('grp', 'ep')), parts along dimension 0, may hold values from 0 to 63, all different within a row; in each aligned block of 64 rows (0 to 63, 64 to 127, ...) at most 8 rows name the same one
- gate_weight: bfloat16 [128, 2048, 384], P('ep', None, 'tp'), may hold values from -0.125 to 0.125
- up_weight: bfloat16 [128, 2048, 384], P('ep', None, 'tp'), may hold values from -0.125 to 0.125
- down_weight: bfloat16 [128, 384, 2048], P('ep', 'tp'), may hold values from -0.21875 to 0.21875
Outputs:
- hidden: bfloat16 [16384, 2048], P(('grp', 'ep'), 'tp'), parts along dimension 0
- expert_out: bfloat16 [16384, 2048], P(('grp', 'ep'), 'tp'), parts along dimension 0
There are 2 independent parts, one for each index of `grp`. A program takes and returns all parts, laid end to end along the dimension named above; an argument that names none is the same for every part. Nothing has to cross between parts.
Inputs may be any that keep to these rules, and one draw needn't show every extreme that they name: `token_request`: in each ep block, 62 tokens belong to request 0, a prefill span, and each other request has exactly one token; the tokens' order in the block is arbitrary. `token_visible`: the span's tokens read consecutive counts s + 1 to s + 62; 512 is reached in every draw. `expert_ids`: each row names 6 different experts; among the 64 tokens of one ep index no expert is named by more than 8 tokens, and this bound is reached.
All inputs are finite; a program needn't handle non-finite values.
Results may differ from a plain program's by a relative error of at most 0.018.
Values may be sent and summed in bfloat16 or wider, within the bound.
A program may use at most 64 MiB of HBM per device.

v0:
```python
import jax
import jax.numpy as jnp
from jax import lax
from jax.sharding import Mesh
from jax.sharding import PartitionSpec as P

LATENT = 512
VDIM = 128
EXPERTS = 64
TOPK = 6
GROUPS = 2
CAP = 8
PIECES = 128
EP = ("ep_0", "ep_1")
GRP_EP = ("grp", "ep_0", "ep_1")
score_scale = 192.0 ** (-0.5)
epsilon = 1e-06


def from_everyone(value, axis):
    peers = lax.axis_size(axis)
    return lax.all_to_all(
        jnp.broadcast_to(value[None], (peers, *value.shape)), axis, 0, 0, tiled=True
    )


def laid_out(pieces, dim):
    lengths = list(pieces.shape[1:])
    lengths[dim] *= pieces.shape[0]
    return jnp.moveaxis(pieces, 0, dim).reshape(lengths)


def collect(value, axis, dim):
    pieces = from_everyone(value, axis)
    return laid_out(pieces, dim)


def of_everyone(value, axis):
    return from_everyone(value, axis).max(axis=0)


def split_up(value, dim, peers):
    before, after = (value.shape[:dim], value.shape[dim + 1 :])
    return jnp.moveaxis(value.reshape(*before, peers, -1, *after), dim, 0)


def sent_and_summed(value, axis, dim):
    peers = lax.axis_size(axis)
    pieces = lax.all_to_all(split_up(value, dim, peers), axis, 0, 0, tiled=True)
    return jnp.sum(pieces, axis=0)


def sent_together(arrays, axis, dim, along):
    columns = [a.reshape(*a.shape[:along], -1) for a in arrays]
    both = jnp.concatenate(columns, axis=along)
    result, at, outs = (sent_and_summed(both, axis, dim), 0, [])
    for a, column in zip(arrays, columns):
        piece = result[..., at : at + column.shape[along]]
        outs.append(piece.reshape(*piece.shape[:along], *a.shape[along:]))
        at += column.shape[along]
    return tuple(outs)


def stacked_from(value, axes, order):
    pieces = value[None]
    for k in order:
        pieces = lax.all_gather(pieces, axes[k], axis=0, tiled=True)
    carried = [lax.axis_size(axes[k]) for k in reversed(order)]
    pieces = pieces.reshape(*carried, *value.shape)
    turned = sorted(range(len(order)), key=lambda place: order[len(order) - 1 - place])
    return pieces.transpose(*turned, *range(len(order), pieces.ndim)).reshape(-1, *value.shape)


def whole_of(value, axes, order, dim):
    return laid_out(stacked_from(value, axes, order), dim)


def over_copies(value, axis):
    everything = from_everyone(value, axis)
    return jnp.sum(everything, axis=0)


def masked_scores(queries, block_rows, token_request, token_visible, offset):
    per_request = block_rows.shape[1]
    flat_rows = block_rows.reshape(-1, block_rows.shape[2])
    scores = (
        jnp.einsum("thc,kc->thk", queries, flat_rows, preferred_element_type=jnp.float32)
        * score_scale
    )
    column = jnp.arange(flat_rows.shape[0], dtype=jnp.int32)
    owner_id = column // per_request
    position = column % per_request + offset
    allowed = (owner_id[None, :] == token_request[:, None]) & (
        position[None, :] < token_visible[:, None]
    )
    return (jnp.where(allowed[:, None, :], scores, -jnp.inf), flat_rows)


def weighted_rows(scores, row_peak, flat_rows):
    weights = jnp.exp(scores - row_peak[:, :, None]).astype(jnp.bfloat16)
    totals = jnp.sum(weights.astype(jnp.float32), axis=2)
    summed = jnp.einsum(
        "thk,kc->thc", weights, flat_rows[:, :LATENT], preferred_element_type=jnp.float32
    )
    return (summed, totals)


def expert_block(arrived, gate_weight, up_weight, down_weight):
    gate_vals = jnp.einsum("prd,pdf->prf", arrived, gate_weight, preferred_element_type=jnp.float32)
    up_vals = jnp.einsum("prd,pdf->prf", arrived, up_weight, preferred_element_type=jnp.float32)
    activated = (jax.nn.silu(gate_vals) * up_vals).astype(jnp.bfloat16)
    return jnp.einsum(
        "prf,pfd->prd", activated, down_weight, preferred_element_type=jnp.float32
    ).astype(jnp.bfloat16)


def body(
    queries,
    latent_cache,
    residual,
    token_request,
    token_visible,
    value_proj,
    out_proj,
    norm_gain,
    router,
    expert_ids,
    gate_weight,
    up_weight,
    down_weight,
):
    all_heads = collect(queries, "tp", 1)
    offset = lax.axis_index("tp") * latent_cache.shape[1]
    scores, flat_rows = masked_scores(all_heads, latent_cache, token_request, token_visible, offset)
    row_peak = of_everyone(jnp.max(scores, axis=2), "tp")
    part_sum, part_total = weighted_rows(scores, row_peak, flat_rows)
    summed, totals = sent_together((part_sum, part_total), "tp", 1, 2)
    context = (summed / totals[:, :, None]).astype(jnp.bfloat16)
    tokens_here = context.shape[0]
    heads_here = context.shape[1]
    head_values = jnp.einsum(
        "thl,hlv->thv",
        context,
        whole_of(value_proj, EP, (0, 1), 1),
        preferred_element_type=jnp.float32,
    )
    heads_out = head_values.astype(jnp.bfloat16).reshape(tokens_here, heads_here * VDIM)
    attention_part = jnp.dot(
        heads_out, whole_of(out_proj, EP, (0, 1), 1), preferred_element_type=jnp.float32
    )
    attention = over_copies(attention_part, "tp")
    hidden = (residual.astype(jnp.float32) + attention).astype(jnp.bfloat16)
    hidden_wide = hidden.astype(jnp.float32)
    normed = (
        hidden_wide
        * lax.rsqrt(jnp.mean(hidden_wide * hidden_wide, axis=1, keepdims=True) + epsilon)
        * norm_gain
    ).astype(jnp.bfloat16)
    logits = jnp.dot(normed, router, preferred_element_type=jnp.float32)
    gate_share = jax.nn.softmax(jnp.take_along_axis(logits, expert_ids, axis=1), axis=1).astype(
        jnp.bfloat16
    )
    flat_ids = expert_ids.reshape(-1)
    position_id = jnp.arange(flat_ids.shape[0], dtype=jnp.int32)
    earlier = (flat_ids[:, None] == flat_ids[None, :]) & (
        position_id[None, :] < position_id[:, None]
    )
    slot_ids = (flat_ids * CAP + jnp.sum(earlier.astype(jnp.int32), axis=1)).reshape(
        tokens_here, TOPK
    )
    targets = jnp.arange(EXPERTS * CAP, dtype=jnp.int32)
    matches = slot_ids[:, :, None] == targets[None, None, :]
    picker = jnp.any(matches, axis=1).T.astype(jnp.bfloat16)
    model_width = normed.shape[1]
    mixing = jnp.sum(
        jnp.where(matches, gate_share[:, :, None], jnp.zeros((), jnp.bfloat16)), axis=1
    )
    mixing = jnp.broadcast_to(
        mixing.reshape(tokens_here, EXPERTS, 1, CAP), (tokens_here, EXPERTS, GROUPS, CAP)
    ).reshape(tokens_here, PIECES * CAP)
    core_count = lax.axis_size("tp")
    half_width = model_width // core_count
    core_start = lax.axis_index("tp") * half_width
    normed_share = lax.dynamic_slice_in_dim(normed, core_start, half_width, 1)
    outgoing = jnp.dot(picker, normed_share, preferred_element_type=jnp.float32).astype(
        jnp.bfloat16
    )
    outgoing = jnp.broadcast_to(
        outgoing.reshape(EXPERTS, 1, CAP, half_width), (EXPERTS, GROUPS, CAP, half_width)
    ).reshape(PIECES, CAP, half_width)
    arrived_share = lax.all_to_all(outgoing, EP, split_axis=0, concat_axis=1, tiled=True)
    arrived = lax.all_gather(arrived_share, "tp", axis=2, tiled=True)
    partial_out = expert_block(arrived, gate_weight, up_weight, down_weight)
    swapped = lax.all_to_all(partial_out[None], "tp", split_axis=3, concat_axis=0, tiled=True)
    returned = lax.all_to_all(swapped, EP, split_axis=2, concat_axis=1, tiled=True)
    returned = returned.reshape(core_count, PIECES * CAP, half_width)
    routed = jnp.einsum("tk,qkd->td", mixing, returned, preferred_element_type=jnp.float32)
    expert_out = routed.astype(jnp.bfloat16)
    hidden_part = lax.dynamic_slice_in_dim(hidden, core_start, half_width, 1)
    return (hidden_part, expert_out)


def solution(mesh):
    finer = Mesh(
        mesh.devices.reshape(mesh.shape["grp"], 8, 16, mesh.shape["tp"]),
        ("grp", "ep_0", "ep_1", "tp"),
    )
    in_specs = (
        P(GRP_EP, "tp", None),
        P(GRP_EP, "tp", None),
        P(GRP_EP, None),
        P(GRP_EP),
        P(GRP_EP),
        P("tp", EP, None),
        P("tp", EP),
        P(),
        P(),
        P(GRP_EP, None),
        P(EP, None, "tp"),
        P(EP, None, "tp"),
        P(EP, "tp", None),
    )
    out_specs = (P(GRP_EP, "tp"), P(GRP_EP, "tp"))
    return jax.shard_map(body, mesh=finer, in_specs=in_specs, out_specs=out_specs, check_vma=False)
```

profile of v0, /device:TPU:320, one launch (start us, length us, event | category | flops | bytes accessed | tf_op | source)
XLA Modules:
  0.0 692.1 jit_solution(127817837888464356)
XLA Ops:
  7.3 26.9 %all-gather = bf16[64,4,128]{2,1,0:T(4,128)(2,1)S(1)} all-gather(bf16[8,4,128]{2,1,0:T(4,128)(2,1)} %param.18), channel_id=2, replica_groups=mesh['grp'=2,'ep_0'=8,'ep_1'=16,'tp'=2] {'ep_0'}, dimensions={0}, use_global_device_ids=true | all-gather | bytes 73728 | tf_op jit(solution)/shard_map/all_gather | solution.py:67
  34.1 0.6 copy.183
  34.9 25.1 %all-gather.1 = bf16[8192,16]{0,1:T(8,128)(2,1)S(1)} all-gather(bf16[1024,16]{0,1:T(8,128)(2,1)} %param.19), channel_id=3, replica_groups=mesh['grp'=2,'ep_0'=8,'ep_1'=16,'tp'=2] {'ep_0'}, dimensions={0}, use_global_device_ids=true | all-gather | bytes 294912 | tf_op jit(solution)/shard_map/all_gather | solution.py:67
  60.0 0.9 copy.205
  61.0 2.3 broadcast_in_dim.49
  63.2 3.7 all-to-all-start
  66.9 1.5 copy.173
  68.6 0.6 all-to-all-done
  69.1 3.2 fusion.4
  72.5 3.7 all_to_all.59
  76.2 0.5 broadcast.146
  76.7 0.7 reduce.3
  77.5 2.9 convert_reduce_fusion.1
  80.8 3.1 convolution_bitcast_fusion
  83.9 1.8 maximum_bitcast_fusion
  85.6 4.0 all-to-all-start.2
  89.7 0.3 all-gather.10.cloned.1.call-start
  90.7 2.2 all-to-all-done.2
  92.9 1.4 reduce_sum.78
  94.2 1.0 slice.16
  95.2 0.4 copy.198
  95.8 1.4 fusion.16
  97.2 36.4 %all-gather.6.cloned.1.call-done = bf16[128,8,4,128]{3,1,2,0:T(8,128)(2,1)} async-done(((bf16[8,8,4,128]{3,1,2,0:T(8,128)(2,1)}), bf16[128,8,4,128]{3,1,2,0:T(8,128)(2,1)}) %all-gather.6.cloned.1.call-update) | async-done | bytes 1048592 | tf_op jit(solution)/shard_map/all_gather | solution.py:67
  133.6 1.8 copy.184
  135.4 0.4 fusion.15
  135.8 76.6 %all-gather.8.cloned.1.call-done = bf16[128,1024,16]{1,0,2:T(8,128)(2,1)} async-done(((bf16[8,1024,16]{1,0,2:T(8,128)(2,1)}), bf16[128,1024,16]{1,0,2:T(8,128)(2,1)}) %all-gather.8.cloned.1.call-update) | async-done | bytes 4194320 | tf_op jit(solution)/shard_map/all_gather | solution.py:67
  212.5 4.5 copy.188
  217.0 1.4 fusion.36
  218.5 4.6 all_to_all.60
  223.5 0.5 fusion.5
  224.3 118.1 %all_to_all.61 = bf16[128,8,1024]{2,1,0:T(8,128)(2,1)} all-to-all(bf16[128,8,1024]{2,1,0:T(8,128)(2,1)S(1)} %bitcast.107), channel_id=1, replica_groups=mesh['grp'=2,'ep_0'=8,'ep_1'=16,'tp'=2] {'ep_0','ep_1'}, dimensions={0} | all-to-all | bytes 4194304 | tf_op jit(solution)/shard_map/all_to_all | solution.py:191
  342.5 14.4 %all-gather.10.cloned.1.call-done = bf16[1,1024,2048]{2,1,0:T(8,128)(2,1)} async-done(((bf16[1,1024,1024]{2,1,0:T(8,128)(2,1)}), bf16[1,1024,2048]{2,1,0:T(8,128)(2,1)}) %all-gather.10.cloned.1.call-update) | async-done | bytes 4194320 | tf_op jit(solution)/shard_map/all_gather | solution.py:192
  356.9 4.6 fusion.2
  361.5 7.3 %convert_bitcast_fusion = bf16[1,1,1024,2048]{3,2,1,0:T(8,128)(2,1)} fusion(bf16[1,192,2048]{2,1,0:T(8,128)(2,1)S(1)} %copy-done, bf16[1,1024,2048]{2,1,0:T(8,128)(2,1)} %all-gather.10.cloned.1.call-done, bf16[1,2048,192]{1,2,0:T(8,128)(2,1)} %param.24, f32[1024,192]{0,1:T(8,128)} %fusion.2), kind=kOutput, calls=%fused_computation.6 | convolution fusion | flops 1613889536 | bytes 10747904 | tf_op jit(solution)/shard_map/prf,pfd->prd/dot_general | solution.py:112
  368.8 20.6 %copy.194 = bf16[1,1,1024,2048]{2,1,0,3:T(2,128)(2,1)} copy(bf16[1,1,1024,2048]{3,2,1,0:T(8,128)(2,1)} %convert_bitcast_fusion) | data formatting | bytes 8388608 | tf_op jit(solution)/shard_map/broadcast_in_dim | solution.py:194
  389.4 0.5 broadcast.147
  389.9 26.0 %reduce.4 = bf16[2048,1024]{1,0:T(8,128)(2,1)} reduce(bf16[2048,1,1,1024]{3,2,1,0:T(2,128)(2,1)} %bitcast.102, bf16[]{:T(256)} %broadcast.147), dimensions={1,2}, to_apply=%bitcast.85.reduce_sub_computation | reduce | bytes 8388610
  415.9 5.9 reshape.241
  421.8 11.9 %all_to_all.62 = bf16[2,2,524288]{2,1,0:T(2,128)(2,1)} all-to-all(bf16[2,2,524288]{2,1,0:T(2,128)(2,1)} %reshape.241), channel_id=1, replica_groups=mesh['grp'=2,'ep_0'=8,'ep_1'=16,'tp'=2] {'tp'}, dimensions={0} | all-to-all | bytes 8388608 | tf_op jit(solution)/shard_map/all_to_all | solution.py:194
  433.7 7.1 %reshape.242 = bf16[2048,1,1,1024]{3,2,1,0:T(2,128)(2,1)} reshape(bf16[2,2,524288]{2,1,0:T(2,128)(2,1)} %all_to_all.62) | data formatting | bytes 8388608
  440.8 7.1 %copy.200 = bf16[1,1,1024,2048]{2,3,0,1:T(8,128)(2,1)} copy(bf16[1,1,1024,2048]{2,1,0,3:T(2,128)(2,1)} %bitcast.103) | data formatting | bytes 8388608
  447.8 11.3 %copy.195 = bf16[2,1,1024,1024]{3,0,1,2:T(2,128)(2,1)} copy(bf16[2,1,1024,1024]{2,3,0,1:T(8,128)(2,1)} %bitcast.104) | data formatting | bytes 8388608 | tf_op jit(solution)/shard_map/all_to_all | solution.py:194
  459.1 21.4 %all-to-all-start.6 = ((bf16[2,1,1024,1024]{3,0,1,2:T(2,128)(2,1)}), bf16[2,1,1024,1024]{3,0,1,2:T(2,128)(2,1)}, u32[]{:S(2)}, u32[]{:S(2)}) async-start(bf16[2,1,1024,1024]{3,0,1,2:T(2,128)(2,1)} %copy.195), calls=%async_computation.6 | async-start | bytes 8388608 | tf_op jit(solution)/shard_map/all_to_all | solution.py:195
  481.0 2.9 gather_fusion
  484.5 0.7 constant_dynamic-slice_fusion
  485.2 186.6 %all-to-all-done.6 = bf16[2,1,1024,1024]{3,0,1,2:T(2,128)(2,1)} async-done(((bf16[2,1,1024,1024]{3,0,1,2:T(2,128)(2,1)}), bf16[2,1,1024,1024]{3,0,1,2:T(2,128)(2,1)}, u32[]{:S(2)}, u32[]{:S(2)}) %all-to-all-start.6) | async-done | bytes 4194336 | tf_op jit(solution)/shard_map/all_to_all | solution.py:195
  671.8 12.4 %convert_reduce_fusion = bf16[1024,1024]{1,0:T(8,128)(2,1)S(1)} fusion(bf16[2,1,1024,1024]{3,0,1,2:T(2,128)(2,1)} %all-to-all-done.6), kind=kLoop, calls=%fused_computation.1 | loop fusion | flops 3145728 | bytes 6291456 | tf_op jit(solution)/shard_map/tk,qkd->td/reduce_sum | solution.py:197
  684.2 1.2 fusion.55
  (58 shorter events, 3.9 us)
Async XLA Ops:
  7.2 354.3 %copy-start = (bf16[1,192,2048]{2,1,0:T(8,128)(2,1)S(1)}, bf16[1,192,2048]{2,1,0:T(8,128)(2,1)}, u32[]{:S(2)}) copy-start(bf16[1,192,2048]{2,1,0:T(8,128)(2,1)} %param.25) | copy-start | bytes 2359300
  7.2 126.4 %all-gather.6.cloned.1.call-start = ((), (), s32[]{:S(2)}) async-start(), calls=%async_computation.7 | async-start | bytes 1114112 | tf_op jit(solution)/shard_map/all_gather | solution.py:67
  34.8 177.6 %all-gather.8.cloned.1.call-start = ((), (), s32[]{:S(2)}) async-start(), calls=%async_computation.8 | async-start | bytes 4456448 | tf_op jit(solution)/shard_map/all_gather | solution.py:67
  60.9 7.5 %copy-start.6 = (s32[64]{0:T(128)S(1)}, s32[64]{0:T(128)}, u32[]{:S(2)}) copy-start(s32[64]{0:T(128)} %param.17) | copy-start | bytes 772
  60.9 7.5 %copy-start.7 = (s32[64]{0:T(128)S(1)}, s32[64]{0:T(128)}, u32[]{:S(2)}) copy-start(s32[64]{0:T(128)} %param.16) | copy-start | bytes 772
  63.2 5.9 all-to-all-start
  85.6 4.4 copy-start.4
  85.6 7.2 %all-to-all-start.2 = ((f32[2,64,8,513]{3,2,1,0:T(8,128)}), f32[2,64,8,513]{3,2,1,0:T(8,128)S(1)}, u32[]{:S(2)}, u32[]{:S(2)}) async-start(f32[2,64,8,513]{3,2,1,0:T(8,128)} %maximum_bitcast_fusion), calls=%async_computation.2 | async-start | bytes 5242880 | tf_op jit(solution)/shard_map/all_to_all | solution.py:49
  89.7 267.2 %all-gather.10.cloned.1.call-start = ((), (), s32[]{:S(2)}) async-start(), calls=%async_computation.9 | async-start | bytes 6291456 | tf_op jit(solution)/shard_map/all_gather | solution.py:192
  218.4 4.8 copy-start.3
  218.4 5.0 copy-start.5
  224.3 132.6 %copy-start.8 = (bf16[1,2048,192]{1,2,0:T(8,128)(2,1)S(1)}, bf16[1,2048,192]{1,2,0:T(8,128)(2,1)}, u32[]{:S(2)}) copy-start(bf16[1,2048,192]{1,2,0:T(8,128)(2,1)} %param.23) | copy-start | bytes 2359300
  459.1 21.7 %copy-start.2 = (bf16[2048,64]{0,1:T(8,128)(2,1)S(1)}, bf16[2048,64]{0,1:T(8,128)(2,1)}, u32[]{:S(2)}) copy-start(bf16[2048,64]{0,1:T(8,128)(2,1)} %param.21) | copy-start | bytes 786436
  459.1 212.7 %all-to-all-start.6 = ((bf16[2,1,1024,1024]{3,0,1,2:T(2,128)(2,1)}), bf16[2,1,1024,1024]{3,0,1,2:T(2,128)(2,1)}, u32[]{:S(2)}, u32[]{:S(2)}) async-start(bf16[2,1,1024,1024]{3,0,1,2:T(2,128)(2,1)} %copy.195), calls=%async_computation.6 | async-start | bytes 8388608 | tf_op jit(solution)/shard_map/all_to_all | solution.py:195
  484.5 200.9 %copy-start.1 = (bf16[1,192,2048]{2,1,0:T(8,128)(2,1)S(1)}, bf16[1,192,2048]{2,1,0:T(8,128)(2,1)}, u32[]{:S(2)}) copy-start(bf16[1,192,2048]{2,1,0:T(8,128)(2,1)} %param.25) | copy-start | bytes 2359300
Sparse Core Ops, SparseCore 0:
  34.9 98.6 all-gather.5
  135.7 76.7 all-gather.7
  342.6 14.2 all-gather.9
where the time goes:
time: 700 us; the launch traced here: 692 us
  waiting for transfers between devices  317 us (45%)
  blocking collectives  190 us (27%)
  local copies, waits for them, and re-layouts  71.6 us (10%)
  other arithmetic  47.6 us (7%)
  starting transfers between devices  29.5 us (4%)
  matrix products  21.9 us (3%)
  between operations  14.3 us (2%)
    all_to_all x1, waiting for transfers between devices, body(): lax.all_to_all(swapped, EP, split_axis=2, concat_axis=1, tiled=True)  187 us
    all_to_all x1, blocking collectives, body(): lax.all_to_all(outgoing, EP, split_axis=0, concat_axis=1, tiled=True)  118 us
    all_gather x2, waiting for transfers between devices, stacked_from(): pieces = lax.all_gather(pieces, axes[k], axis=0, tiled=True)  113 us
    all_gather x2, blocking collectives, stacked_from(): pieces = lax.all_gather(pieces, axes[k], axis=0, tiled=True)  52 us
    unnamed x1, other arithmetic  26 us
    unnamed x28, local copies, waits for them, and re-layouts  23.3 us
    all_to_all x1, starting transfers between devices, body(): lax.all_to_all(swapped, EP, split_axis=2, concat_axis=1, tiled=True)  21.4 us
    broadcast_in_dim x1, local copies, waits for them, and re-layouts, body(): partial_out[None]  20.6 us
  transfers between devices with their start and end apart: 6, of which 6 were waited for; matrix products, arithmetic and copies ran while one was open for 4% of the time, Pallas kernels for 0%

commit v1 on v0

--- a/solution.py
+++ b/solution.py
@@ -64,7 +64,9 @@
 def stacked_from(value, axes, order):
     pieces = value[None]
     for k in order:
-        pieces = lax.all_gather(pieces, axes[k], axis=0, tiled=True)
+        pieces = jnp.concatenate(
+            lax.all_to_all(jnp.stack([pieces] * lax.axis_size(axes[k])), axes[k], 0, 0), axis=0
+        )
     carried = [lax.axis_size(axes[k]) for k in reversed(order)]
     pieces = pieces.reshape(*carried, *value.shape)
     turned = sorted(range(len(order)), key=lambda place: order[len(order) - 1 - place])

time: 700 us -> 827 us (1.18)
  waiting for transfers between devices: 317 us -> 388 us
  blocking collectives: 190 us -> 246 us
    all_to_all x1 -> x2, waiting for transfers between devices: 2.18 us -> 185 us  [stacked_from(): lax.all_to_all(jnp.stack([pieces] * lax.axis_size(axes[k])), axes[k], 0, 0)]
    all_gather x2 -> x0, waiting for transfers between devices: 113 us -> none  [stacked_from(): pieces = lax.all_gather(pieces, axes[k], axis=0, tiled=True)]
    all_to_all x0 -> x3, blocking collectives: none -> 108 us  [the longest x2 102 us: stacked_from(): lax.all_to_all(jnp.stack([pieces] * lax.axis_size(axes[k])), axes[k], 0, 0)]
    all_gather x2 -> x0, blocking collectives: 52 us -> none  [stacked_from(): pieces = lax.all_gather(pieces, axes[k], axis=0, tiled=True)]
    unnamed x28 -> x37, local copies, waits for them, and re-layouts: 23.3 us -> 22.4 us
  transfers between devices with their start and end apart: 6 -> 5, of which waited for: 6 -> 5; matrix products, arithmetic and copies ran while one was open for 4% -> 2% of each run, Pallas kernels for 0% -> 0%
where the time goes in v1:
time: 827 us; the launch traced here: 825 us
  waiting for transfers between devices  388 us (47%)
  blocking collectives  246 us (30%)
  local copies, waits for them, and re-layouts  72.2 us (9%)
  other arithmetic  46.3 us (6%)
  starting transfers between devices  36.7 us (4%)
  matrix products  21.1 us (3%)
  between operations  14.5 us (2%)
    all_to_all x1, waiting for transfers between devices, body(): lax.all_to_all(swapped, EP, split_axis=2, concat_axis=1, tiled=True)  187 us
    all_to_all x2, waiting for transfers between devices, stacked_from(): lax.all_to_all(jnp.stack([pieces] * lax.axis_size(axes[k])), axes[k], 0, 0)  185 us
    all_to_all x1, blocking collectives, body(): lax.all_to_all(outgoing, EP, split_axis=0, concat_axis=1, tiled=True)  118 us
    all_to_all x2, blocking collectives, stacked_from(): lax.all_to_all(jnp.stack([pieces] * lax.axis_size(axes[k])), axes[k], 0, 0)  102 us
    unnamed x1, other arithmetic  26 us
    unnamed x37, local copies, waits for them, and re-layouts  22.4 us
    all_to_all x1, starting transfers between devices, body(): lax.all_to_all(swapped, EP, split_axis=2, concat_axis=1, tiled=True)  21.2 us
    broadcast_in_dim x1, local copies, waits for them, and re-layouts, body(): partial_out[None]  20.6 us
  transfers between devices with their start and end apart: 5, of which 5 were waited for; matrix products, arithmetic and copies ran while one was open for 2% of the time, Pallas kernels for 0%

profile of v1, /device:TPU:320, one launch (start us, length us, event | category | flops | bytes accessed | tf_op | source)
XLA Modules:
  0.0 824.6 jit_solution(3625868325850252847)
XLA Ops:
  7.2 2.3 broadcast_in_dim.45
  9.5 3.7 all-to-all-start
  13.2 1.5 copy.139
  14.9 0.6 all-to-all-done
  15.5 3.1 fusion.4
  18.8 3.7 all_to_all.79
  22.5 0.5 broadcast.152
  23.0 0.7 reduce.3
  23.9 3.0 convert_reduce_fusion.1
  26.9 2.4 convolution_bitcast_fusion
  29.9 5.9 all_to_all.80
  35.7 15.5 %all_to_all.81 = bf16[8,1,8,4,128]{4,3,2,1,0:T(4,128)(2,1)S(1)} all-to-all(bf16[8,1,8,4,128]{4,3,2,1,0:T(4,128)(2,1)S(1)} %stack.12), channel_id=1, replica_groups=mesh['grp'=2,'ep_0'=8,'ep_1'=16,'tp'=2] {'ep_0'}, dimensions={0} | all-to-all | bytes 131072 | tf_op jit(solution)/shard_map/all_to_all | solution.py:68
  51.3 0.7 stack.14
  52.0 4.2 all-to-all-start.5
  56.2 10.8 %all-to-all-done.5 = bf16[8,1,1024,16]{2,3,1,0:T(8,128)(2,1)} async-done(((bf16[8,1,1024,16]{2,3,1,0:T(8,128)(2,1)}), bf16[8,1,1024,16]{2,3,1,0:T(8,128)(2,1)}, u32[]{:S(2)}, u32[]{:S(2)}) %all-to-all-start.5) | async-done | bytes 262176 | tf_op jit(solution)/shard_map/all_to_all | solution.py:68
  67.1 0.4 stack.13
  67.5 86.5 %all_to_all.82 = bf16[16,8,8,4,128]{4,3,1,2,0:T(4,128)(2,1)} all-to-all(bf16[16,8,8,4,128]{4,3,1,2,0:T(4,128)(2,1)S(1)} %stack.13), channel_id=1, replica_groups=mesh['grp'=2,'ep_0'=8,'ep_1'=16,'tp'=2] {'ep_1'}, dimensions={0} | all-to-all | bytes 2097152 | tf_op jit(solution)/shard_map/all_to_all | solution.py:68
  154.0 3.4 stack.15
  157.4 7.5 all-to-all-start.6
  165.7 1.5 reduce_sum.78
  167.2 1.1 slice.16
  168.2 0.4 copy.164
  168.9 1.4 fusion.16
  170.3 0.7 copy.150
  170.9 0.4 copy.151
  171.7 174.2 %all-to-all-done.6 = bf16[16,8,1024,16]{2,3,1,0:T(8,128)(2,1)} async-done(((bf16[16,8,1024,16]{2,3,1,0:T(8,128)(2,1)}), bf16[16,8,1024,16]{2,3,1,0:T(8,128)(2,1)}, u32[]{:S(2)}, u32[]{:S(2)}) %all-to-all-start.6) | async-done | bytes 4194336 | tf_op jit(solution)/shard_map/all_to_all | solution.py:68
  346.0 2.6 copy.154
  348.6 1.4 fusion.36
  350.1 4.6 all_to_all.83
  355.2 0.5 fusion.5
  355.9 117.8 %all_to_all.84 = bf16[128,8,1024]{2,1,0:T(8,128)(2,1)} all-to-all(bf16[128,8,1024]{2,1,0:T(8,128)(2,1)S(1)} %bitcast.101), channel_id=1, replica_groups=mesh['grp'=2,'ep_0'=8,'ep_1'=16,'tp'=2] {'ep_0','ep_1'}, dimensions={0} | all-to-all | bytes 4194304 | tf_op jit(solution)/shard_map/all_to_all | solution.py:193
  473.8 15.7 %all-gather.2.cloned.1.call-done = bf16[1,1024,2048]{2,1,0:T(8,128)(2,1)} async-done(((bf16[1,1024,1024]{2,1,0:T(8,128)(2,1)}), bf16[1,1024,2048]{2,1,0:T(8,128)(2,1)}) %all-gather.2.cloned.1.call-update) | async-done | bytes 4194320 | tf_op jit(solution)/shard_map/all_gather | solution.py:194
  489.4 4.6 fusion.2
  494.0 7.3 convert_bitcast_fusion
  501.3 20.6 %copy.160 = bf16[1,1,1024,2048]{2,1,0,3:T(2,128)(2,1)} copy(bf16[1,1,1024,2048]{3,2,1,0:T(8,128)(2,1)} %convert_bitcast_fusion) | data formatting | bytes 8388608 | tf_op jit(solution)/shard_map/broadcast_in_dim | solution.py:196
  521.9 0.5 broadcast.153
  522.4 26.0 %reduce.4 = bf16[2048,1024]{1,0:T(8,128)(2,1)} reduce(bf16[2048,1,1,1024]{3,2,1,0:T(2,128)(2,1)} %bitcast.96, bf16[]{:T(256)} %broadcast.153), dimensions={1,2}, to_apply=%bitcast.79.reduce_sub_computation | reduce | bytes 8388610
  548.4 5.9 reshape.239
  554.3 11.9 %all_to_all.85 = bf16[2,2,524288]{2,1,0:T(2,128)(2,1)} all-to-all(bf16[2,2,524288]{2,1,0:T(2,128)(2,1)} %reshape.239), channel_id=1, replica_groups=mesh['grp'=2,'ep_0'=8,'ep_1'=16,'tp'=2] {'tp'}, dimensions={0} | all-to-all | bytes 8388608 | tf_op jit(solution)/shard_map/all_to_all | solution.py:196
  566.2 7.1 reshape.240
  573.3 7.1 copy.165
  580.3 11.3 %copy.161 = bf16[2,1,1024,1024]{3,0,1,2:T(2,128)(2,1)} copy(bf16[2,1,1024,1024]{2,3,0,1:T(8,128)(2,1)} %bitcast.98) | data formatting | bytes 8388608 | tf_op jit(solution)/shard_map/all_to_all | solution.py:196
  591.7 21.2 %all-to-all-start.10 = ((bf16[2,1,1024,1024]{3,0,1,2:T(2,128)(2,1)}), bf16[2,1,1024,1024]{3,0,1,2:T(2,128)(2,1)}, u32[]{:S(2)}, u32[]{:S(2)}) async-start(bf16[2,1,1024,1024]{3,0,1,2:T(2,128)(2,1)} %copy.161), calls=%async_computation.10 | async-start | bytes 8388608 | tf_op jit(solution)/shard_map/all_to_all | solution.py:197
  613.4 2.9 gather_fusion
  616.9 0.7 constant_dynamic-slice_fusion
  617.5 186.6 %all-to-all-done.10 = bf16[2,1,1024,1024]{3,0,1,2:T(2,128)(2,1)} async-done(((bf16[2,1,1024,1024]{3,0,1,2:T(2,128)(2,1)}), bf16[2,1,1024,1024]{3,0,1,2:T(2,128)(2,1)}, u32[]{:S(2)}, u32[]{:S(2)}) %all-to-all-start.10) | async-done | bytes 4194336 | tf_op jit(solution)/shard_map/all_to_all | solution.py:197
  804.2 12.4 %convert_reduce_fusion = bf16[1024,1024]{1,0:T(8,128)(2,1)S(1)} fusion(bf16[2,1,1024,1024]{3,0,1,2:T(2,128)(2,1)} %all-to-all-done.10), kind=kLoop, calls=%fused_computation.1 | loop fusion | flops 3145728 | bytes 6291456 | tf_op jit(solution)/shard_map/tk,qkd->td/reduce_sum | solution.py:199
  816.6 1.2 fusion.55
  (69 shorter events, 4.3 us)
Async XLA Ops:
  7.2 486.9 %copy-start = (bf16[1,192,2048]{2,1,0:T(8,128)(2,1)S(1)}, bf16[1,192,2048]{2,1,0:T(8,128)(2,1)}, u32[]{:S(2)}) copy-start(bf16[1,192,2048]{2,1,0:T(8,128)(2,1)} %param.25) | copy-start | bytes 2359300
  7.2 7.6 copy-start.11
  7.2 7.6 copy-start.12
  9.5 5.9 all-to-all-start
  14.8 3.9 copy-start.4
  23.9 3.0 copy-start.3
  29.8 5.9 copy-start.10
  29.9 21.4 %copy-start.8 = (bf16[1024,16]{0,1:T(8,128)(2,1)S(1)}, bf16[1024,16]{0,1:T(8,128)(2,1)}, u32[]{:S(2)}) copy-start(bf16[1024,16]{0,1:T(8,128)(2,1)} %param.19) | copy-start | bytes 98308
  52.0 15.1 %all-to-all-start.5 = ((bf16[8,1,1024,16]{2,3,1,0:T(8,128)(2,1)}), bf16[8,1,1024,16]{2,3,1,0:T(8,128)(2,1)}, u32[]{:S(2)}, u32[]{:S(2)}) async-start(bf16[8,1,1024,16]{2,3,1,0:T(8,128)(2,1)} %stack.14), calls=%async_computation.5 | async-start | bytes 524288 | tf_op jit(solution)/shard_map/all_to_all | solution.py:68
  157.4 7.6 copy-start.7
  157.4 188.6 %all-to-all-start.6 = ((bf16[16,8,1024,16]{2,3,1,0:T(8,128)(2,1)}), bf16[16,8,1024,16]{2,3,1,0:T(8,128)(2,1)}, u32[]{:S(2)}, u32[]{:S(2)}) async-start(bf16[16,8,1024,16]{2,3,1,0:T(8,128)(2,1)} %stack.15), calls=%async_computation.6 | async-start | bytes 8388608 | tf_op jit(solution)/shard_map/all_to_all | solution.py:68
  164.9 324.5 %all-gather.2.cloned.1.call-start = ((), (), s32[]{:S(2)}) async-start(), calls=%async_computation.11 | async-start | bytes 6291456 | tf_op jit(solution)/shard_map/all_gather | solution.py:194
  167.2 3.1 copy-start.2
  350.0 4.8 copy-start.6
  350.0 5.0 copy-start.9
  355.9 133.5 %copy-start.13 = (bf16[1,2048,192]{1,2,0:T(8,128)(2,1)S(1)}, bf16[1,2048,192]{1,2,0:T(8,128)(2,1)}, u32[]{:S(2)}) copy-start(bf16[1,2048,192]{1,2,0:T(8,128)(2,1)} %param.23) | copy-start | bytes 2359300
  591.6 21.5 %copy-start.5 = (bf16[2048,64]{0,1:T(8,128)(2,1)S(1)}, bf16[2048,64]{0,1:T(8,128)(2,1)}, u32[]{:S(2)}) copy-start(bf16[2048,64]{0,1:T(8,128)(2,1)} %param.21) | copy-start | bytes 786436
  591.7 212.5 %all-to-all-start.10 = ((bf16[2,1,1024,1024]{3,0,1,2:T(2,128)(2,1)}), bf16[2,1,1024,1024]{3,0,1,2:T(2,128)(2,1)}, u32[]{:S(2)}, u32[]{:S(2)}) async-start(bf16[2,1,1024,1024]{3,0,1,2:T(2,128)(2,1)} %copy.161), calls=%async_computation.10 | async-start | bytes 8388608 | tf_op jit(solution)/shard_map/all_to_all | solution.py:197
  616.9 200.9 %copy-start.1 = (bf16[1,192,2048]{2,1,0:T(8,128)(2,1)S(1)}, bf16[1,192,2048]{2,1,0:T(8,128)(2,1)}, u32[]{:S(2)}) copy-start(bf16[1,192,2048]{2,1,0:T(8,128)(2,1)} %param.25) | copy-start | bytes 2359300
Sparse Core Ops, SparseCore 0:
  473.9 15.4 all-gather.1
